TPU v7x, 32 devices: a whole 2x2x4 slice. The times are simulated.
32 devices in a mesh: exp: 8 (over y, x, core), tp: 4 (over z).
Axes of the slice: x: 2, y: 2, z: 4, core: 2. Of those that a mesh axis runs over, the one named last changes fastest.
Arguments:
- tokens: bfloat16 [224, 4096], P('exp', 'tp'), may hold values from -6 to 6
- cotangent: bfloat16 [224, 4096], P('exp', 'tp'), may hold values from -6 to 6
- experts: int32 [224, 2], P('exp'), may hold values from 0 to 7, all different within a row; in each aligned block of 28 rows (0 to 27, 28 to 55, ...) at most 8 rows name the same one
- gates: float32 [224, 2], P('exp'), may hold values from 0.1 to 0.9
- w_gate: bfloat16 [8, 4096, 8192], P('exp', None, 'tp'), may hold values from -0.09375 to 0.09375
- w_up: bfloat16 [8, 4096, 8192], P('exp', None, 'tp'), may hold values from -0.09375 to 0.09375
- w_down: bfloat16 [8, 8192, 4096], P('exp', 'tp'), may hold values from -0.0625 to 0.0625
Outputs:
- output: bfloat16 [224, 4096], P('exp', 'tp')
- input_grad: bfloat16 [224, 4096], P('exp', 'tp')
- grad_gate: bfloat16 [8, 4096, 8192], P('exp', None, 'tp')
- grad_up: bfloat16 [8, 4096, 8192], P('exp', None, 'tp')
- grad_down: bfloat16 [8, 8192, 4096], P('exp', 'tp')
Inputs may be any that keep to these rules, and one draw needn't show every extreme that they name: Each row names 2 different experts. In each aligned block of 28 rows (the rows of one index of exp) no expert is named by more than 8 rows, and in some blocks one is named by exactly 8.
All inputs are finite; a program needn't handle non-finite values.
Results may differ from a plain program's by a relative error of at most 0.017.
Values may be sent and summed in bfloat16 or wider, within the bound.
A program may use at most 192 MiB of HBM per device.

v0:
```python
import jax
import jax.numpy as jnp
from jax import lax
from jax.sharding import PartitionSpec as P

EXPERTS = 8
CAP = 8


def contract_rows(left, right):
    return lax.dot_general(
        left, right, (((0,), (0,)), ((), ())), preferred_element_type=jnp.float32
    )


def contract_cols(left, right):
    return lax.dot_general(
        left, right, (((1,), (1,)), ((), ())), preferred_element_type=jnp.float32
    )


def slot_places(experts, capacity):
    pair_ids = experts.reshape(-1)
    matches = (pair_ids[:, None] == jnp.arange(EXPERTS, dtype=jnp.int32)[None, :]).astype(jnp.int32)
    before = jnp.cumsum(matches, axis=0) - matches
    slot_ids = jnp.sum(before * matches, axis=1)
    return pair_ids * capacity + slot_ids


def per_device(tokens, cotangent, experts, gates, w_gate, w_up, w_down):
    exp_devices = lax.axis_size("exp")
    group_size = exp_devices // EXPERTS
    capacity = CAP
    tok_rows, top_count = experts.shape
    model_width = w_gate.shape[1]
    gate_mat = w_gate[0]
    up_mat = w_up[0]
    down_mat = w_down[0]
    row_count = exp_devices * capacity
    places = slot_places(experts, capacity)
    pick_table = (
        places[:, None] == jnp.arange(EXPERTS * capacity, dtype=jnp.int32)[None, :]
    ).astype(jnp.float32)
    per_token = pick_table.reshape(tok_rows, top_count, EXPERTS * capacity)
    weighted = jnp.sum(per_token * gates[:, :, None], axis=1)
    unweighted = jnp.sum(per_token, axis=1)
    pick_low = pick_table.astype(jnp.bfloat16)
    scaled = (gates[:, :, None] * cotangent[:, None, :].astype(jnp.float32)).astype(jnp.bfloat16)
    scaled = scaled.reshape(tok_rows * top_count, cotangent.shape[1])

    def merge_group(received):
        col_count = received.shape[2]
        summed = jnp.sum(received.reshape(EXPERTS, group_size, capacity, col_count), axis=1)
        return summed.reshape(EXPERTS * capacity, col_count)

    def gather_tokens(table, received):
        return jnp.dot(
            table,
            merge_group(received),
            precision=lax.Precision.HIGHEST,
            preferred_element_type=jnp.float32,
        )

    whole_tokens, whole_scaled = (
        lax.all_gather(tokens, "tp", axis=1, tiled=True),
        lax.all_gather(scaled, "tp", axis=1, tiled=True),
    )
    col_count = whole_tokens.shape[1]
    repeated = jnp.repeat(whole_tokens, top_count, axis=0)
    token_send = contract_rows(pick_low, repeated).astype(jnp.bfloat16)
    grad_send = contract_rows(pick_low, whole_scaled).astype(jnp.bfloat16)
    token_send = jnp.broadcast_to(
        token_send.reshape(EXPERTS, 1, capacity, col_count),
        (EXPERTS, group_size, capacity, col_count),
    )
    grad_send = jnp.broadcast_to(
        grad_send.reshape(EXPERTS, 1, capacity, col_count),
        (EXPERTS, group_size, capacity, col_count),
    )
    token_send, grad_send = (
        token_send.reshape(exp_devices, capacity, col_count),
        grad_send.reshape(exp_devices, capacity, col_count),
    )
    token_rows, cot_rows = (
        lax.all_to_all(token_send, "exp", split_axis=0, concat_axis=0, tiled=True),
        lax.all_to_all(grad_send, "exp", split_axis=0, concat_axis=0, tiled=True),
    )
    token_rows = token_rows.reshape(row_count, model_width)
    cot_rows = cot_rows.reshape(row_count, model_width)
    hidden_gate = jnp.dot(token_rows, gate_mat, preferred_element_type=jnp.float32)
    hidden_up = jnp.dot(token_rows, up_mat, preferred_element_type=jnp.float32)
    grad_act = contract_cols(cot_rows, down_mat)
    sigmoid_gate = jax.nn.sigmoid(hidden_gate)
    activation = (hidden_gate * sigmoid_gate * hidden_up).astype(jnp.bfloat16)
    out_term = jnp.dot(activation, down_mat, preferred_element_type=jnp.float32)
    grad_first = (
        grad_act * hidden_up * sigmoid_gate * (1.0 + hidden_gate * (1.0 - sigmoid_gate))
    ).astype(jnp.bfloat16)
    grad_second = (grad_act * hidden_gate * sigmoid_gate).astype(jnp.bfloat16)
    grad_down = contract_rows(activation, cot_rows).astype(jnp.bfloat16)
    grad_gate = contract_rows(token_rows, grad_first).astype(jnp.bfloat16)
    grad_up = contract_rows(token_rows, grad_second).astype(jnp.bfloat16)
    back_term = contract_cols(grad_first, gate_mat) + contract_cols(grad_second, up_mat)
    out_back, grad_back = (
        lax.all_to_all(
            out_term.reshape(exp_devices, capacity, model_width),
            "exp",
            split_axis=0,
            concat_axis=0,
            tiled=True,
        ),
        lax.all_to_all(
            back_term.reshape(exp_devices, capacity, model_width),
            "exp",
            split_axis=0,
            concat_axis=0,
            tiled=True,
        ),
    )
    out_tokens = gather_tokens(weighted, out_back)
    grad_tokens = gather_tokens(unweighted, grad_back)
    output, input_grad = (
        lax.psum_scatter(
            out_tokens.astype(jnp.bfloat16), "tp", scatter_dimension=1, tiled=True
        ).astype(jnp.float32),
        lax.psum_scatter(
            grad_tokens.astype(jnp.bfloat16), "tp", scatter_dimension=1, tiled=True
        ).astype(jnp.float32),
    )
    return (
        output.astype(jnp.bfloat16),
        input_grad.astype(jnp.bfloat16),
        grad_gate[None],
        grad_up[None],
        grad_down[None],
    )


def solution(mesh):
    in_specs = (
        P("exp", "tp"),
        P("exp", "tp"),
        P("exp", None),
        P("exp", None),
        P("exp", None, "tp"),
        P("exp", None, "tp"),
        P("exp", "tp", None),
    )
    out_specs = (
        P("exp", "tp"),
        P("exp", "tp"),
        P("exp", None, "tp"),
        P("exp", None, "tp"),
        P("exp", "tp", None),
    )
    return jax.shard_map(
        per_device, mesh=mesh, in_specs=in_specs, out_specs=out_specs, check_vma=False
    )
```

profile of v0, /device:TPU:0, one launch (start us, length us, event | category | flops | bytes accessed | tf_op | source)
XLA Modules:
  0.0 172.2 jit_solution(9109463998063205250)
XLA Ops:
  7.2 0.8 copy.30
  8.0 0.8 copy.27
  9.3 0.9 mul.79
  10.4 16.8 %all_gather.7 = bf16[56,4096]{1,0:T(8,128)(2,1)S(1)} all-gather(bf16[56,1024]{1,0:T(8,128)(2,1)S(1)} %multiply_convert_fusion.3), channel_id=1, replica_groups=mesh['exp'=8,'tp'=4] {'tp'}, dimensions={1}, use_global_device_ids=true | all-gather | bytes 573440 | tf_op jit(solution)/shard_map/all_gather | solution.py:66
  27.2 1.2 fusion.19
  28.4 3.7 %all-to-all-start.2 = ((bf16[8,8,4096]{2,1,0:T(8,128)(2,1)}), bf16[8,8,4096]{2,1,0:T(8,128)(2,1)S(1)}, u32[]{:S(2)}, u32[]{:S(2)}) async-start(bf16[8,8,4096]{2,1,0:T(8,128)(2,1)} %fusion.19), calls=%async_computation.3 | async-start | bytes 1048576 | tf_op jit(solution)/shard_map/all_to_all | solution.py:86
  32.3 14.9 %all_gather.6 = bf16[28,4096]{1,0:T(8,128)(2,1)S(1)} all-gather(bf16[28,1024]{1,0:T(8,128)(2,1)} %param.7), channel_id=1, replica_groups=mesh['exp'=8,'tp'=4] {'tp'}, dimensions={1}, use_global_device_ids=true | all-gather | bytes 286720 | tf_op jit(solution)/shard_map/all_gather | solution.py:65
  47.8 1.2 fusion.18
  49.0 3.9 %all-to-all-start = ((bf16[8,8,4096]{2,1,0:T(8,128)(2,1)}), bf16[8,8,4096]{2,1,0:T(8,128)(2,1)S(1)}, u32[]{:S(2)}, u32[]{:S(2)}) async-start(bf16[8,8,4096]{2,1,0:T(8,128)(2,1)} %fusion.18), calls=%async_computation | async-start | bytes 1048576 | tf_op jit(solution)/shard_map/all_to_all | solution.py:85
  52.9 11.0 %fusion.2 = f32[64,2048]{1,0:T(8,128)S(1)} fusion(bf16[1,2048,4096]{2,1,0:T(8,128)(2,1)} %param.13, bf16[8,8,4096]{2,1,0:T(8,128)(2,1)S(1)} %all-to-all-done.2), kind=kOutput, calls=%fused_computation.2 | convolution fusion | flops 1073741824 | bytes 17825792 | tf_op jit(solution)/shard_map/dot_general | solution.py:17
  63.9 8.9 %fusion.6 = f32[64,2048]{1,0:T(8,128)S(1)} fusion(bf16[1,4096,2048]{2,1,0:T(8,128)(2,1)} %param.12, bf16[8,8,4096]{2,1,0:T(8,128)(2,1)S(1)} %all-to-all-done), kind=kOutput, calls=%fused_computation.6 | convolution fusion | flops 1073741824 | bytes 17825792 | tf_op jit(solution)/shard_map/dot_general | solution.py:91
  72.9 10.0 %multiply_convert_fusion.1 = (bf16[64,2048]{1,0:T(8,128)(2,1)}, bf16[64,2048]{1,0:T(8,128)(2,1)S(1)}, bf16[64,2048]{1,0:T(8,128)(2,1)}) fusion(f32[64,2048]{1,0:T(8,128)S(1)} %fusion.2, f32[64,2048]{1,0:T(8,128)S(1)} %fusion.6, bf16[1,4096,2048]{2,1,0:T(8,128)(2,1)} %param.11, bf16[8,8,4096]{2,1,0:T(8,128)(2,1)S(1)} %all-to-all-done), kind=kOutput, calls=%fused_computation.32 | convolution fusion | flops 1075838976 | bytes 19136512 | tf_op jit(solution)/shard_map/dot_general | solution.py:90
  82.9 4.0 %fusion = f32[8,8,4096]{2,1,0:T(8,128)} fusion(bf16[1,2048,4096]{2,1,0:T(8,128)(2,1)S(1)} %bitcast.69, bf16[64,2048]{1,0:T(8,128)(2,1)S(1)} %get-tuple-element.8), kind=kOutput, calls=%fused_computation | convolution fusion | flops 1073741824 | bytes 18087936 | tf_op jit(solution)/shard_map/dot_general | solution.py:95
  86.9 4.2 %all-to-all-start.1 = ((f32[8,8,4096]{2,1,0:T(8,128)}), f32[8,8,4096]{2,1,0:T(8,128)S(1)}, u32[]{:S(2)}, u32[]{:S(2)}) async-start(f32[8,8,4096]{2,1,0:T(8,128)} %fusion), calls=%async_computation.1 | async-start | bytes 2097152 | tf_op jit(solution)/shard_map/all_to_all | solution.py:105
  91.1 11.0 %fusion.4 = f32[64,4096]{1,0:T(8,128)S(1)} fusion(bf16[64,2048]{1,0:T(8,128)(2,1)} %get-tuple-element.9, bf16[1,4096,2048]{2,1,0:T(8,128)(2,1)} %param.12), kind=kOutput, calls=%fused_computation.4 | convolution fusion | flops 1073741824 | bytes 18087936 | tf_op jit(solution)/shard_map/dot_general | solution.py:17
  102.2 12.0 %fusion.15 = f32[8,8,4096]{2,1,0:T(8,128)} fusion(f32[64,4096]{1,0:T(8,128)S(1)} %fusion.4, bf16[64,2048]{1,0:T(8,128)(2,1)} %get-tuple-element.7, bf16[1,4096,2048]{2,1,0:T(8,128)(2,1)} %param.11), kind=kOutput, calls=%fused_computation.16 | convolution fusion | flops 1074003968 | bytes 19136512 | tf_op jit(solution)/shard_map/dot_general | solution.py:17
  114.2 4.2 %all-to-all-start.3 = ((f32[8,8,4096]{2,1,0:T(8,128)}), f32[8,8,4096]{2,1,0:T(8,128)S(1)}, u32[]{:S(2)}, u32[]{:S(2)}) async-start(f32[8,8,4096]{2,1,0:T(8,128)} %fusion.15), calls=%async_computation.4 | async-start | bytes 2097152 | tf_op jit(solution)/shard_map/all_to_all | solution.py:112
  118.7 1.3 convolution_convert_fusion.3
  120.4 9.5 %convert_bitcast_fusion.2 = bf16[1,4096,2048]{2,1,0:T(8,128)(2,1)} fusion(bf16[64,2048]{1,0:T(8,128)(2,1)} %get-tuple-element.7, bf16[8,8,4096]{2,1,0:T(8,128)(2,1)S(1)} %all-to-all-done), kind=kOutput, calls=%fused_computation.14 | convolution fusion | flops 1082130432 | bytes 17563648 | tf_op jit(solution)/shard_map/dot_general | solution.py:11
  129.9 3.9 %all-to-all-done.3 = f32[8,8,4096]{2,1,0:T(8,128)S(1)} async-done(((f32[8,8,4096]{2,1,0:T(8,128)}), f32[8,8,4096]{2,1,0:T(8,128)S(1)}, u32[]{:S(2)}, u32[]{:S(2)}) %all-to-all-start.3) | async-done | bytes 1048608 | tf_op jit(solution)/shard_map/all_to_all | solution.py:112
  133.8 1.3 convolution_convert_fusion.2
  135.1 8.5 %convert_bitcast_fusion.1 = bf16[1,4096,2048]{2,1,0:T(8,128)(2,1)} fusion(bf16[64,2048]{1,0:T(8,128)(2,1)S(1)} %copy-done, bf16[8,8,4096]{2,1,0:T(8,128)(2,1)S(1)} %all-to-all-done), kind=kOutput, calls=%fused_computation.13 | convolution fusion | flops 1082130432 | bytes 17563648 | tf_op jit(solution)/shard_map/dot_general | solution.py:11
  143.7 8.5 %convert_bitcast_fusion = bf16[1,2048,4096]{2,1,0:T(8,128)(2,1)} fusion(bf16[64,2048]{1,0:T(8,128)(2,1)S(1)} %get-tuple-element.8, bf16[8,8,4096]{2,1,0:T(8,128)(2,1)S(1)} %all-to-all-done.2), kind=kOutput, calls=%fused_computation.12 | convolution fusion | flops 1082130432 | bytes 17563648 | tf_op jit(solution)/shard_map/dot_general | solution.py:11
  152.2 13.1 %reduce-scatter.5.cloned.1.call-done = bf16[28,1024]{1,0:T(8,128)(2,1)} async-done(((bf16[28,4096]{1,0:T(8,128)(2,1)}), bf16[28,1024]{1,0:T(8,128)(2,1)}) %reduce-scatter.5.cloned.1.call-update) | async-done | bytes 57360 | tf_op jit(solution)/shard_map/reduce_scatter | solution.py:126
  (36 shorter events, 2.2 us)
Async XLA Ops:
  28.4 20.6 %all-to-all-start.2 = ((bf16[8,8,4096]{2,1,0:T(8,128)(2,1)}), bf16[8,8,4096]{2,1,0:T(8,128)(2,1)S(1)}, u32[]{:S(2)}, u32[]{:S(2)}) async-start(bf16[8,8,4096]{2,1,0:T(8,128)(2,1)} %fusion.19), calls=%async_computation.3 | async-start | bytes 1048576 | tf_op jit(solution)/shard_map/all_to_all | solution.py:86
  49.0 14.9 %all-to-all-start = ((bf16[8,8,4096]{2,1,0:T(8,128)(2,1)}), bf16[8,8,4096]{2,1,0:T(8,128)(2,1)S(1)}, u32[]{:S(2)}, u32[]{:S(2)}) async-start(bf16[8,8,4096]{2,1,0:T(8,128)(2,1)} %fusion.18), calls=%async_computation | async-start | bytes 1048576 | tf_op jit(solution)/shard_map/all_to_all | solution.py:85
  63.9 18.9 %slice-start = ((s8[16777216]{0:T(1024)(128)(4,1)}), s8[4194304]{0:T(1024)(128)(4,1)S(1)}, s32[]{:S(2)}) async-start(s8[16777216]{0:T(1024)(128)(4,1)} %bitcast.68), calls=%async_computation.8 | async-start | bytes 8388608
  63.9 18.9 %slice-start.1 = ((s8[16777216]{0:T(1024)(128)(4,1)}), s8[4194304]{0:T(1024)(128)(4,1)S(1)}, s32[]{:S(2)}) async-start(s8[16777216]{0:T(1024)(128)(4,1)} %bitcast.68), calls=%async_computation.9 | async-start | bytes 8388608
  72.9 10.0 %slice-start.2 = ((s8[16777216]{0:T(1024)(128)(4,1)}), s8[4194304]{0:T(1024)(128)(4,1)S(1)}, s32[]{:S(2)}) async-start(s8[16777216]{0:T(1024)(128)(4,1)} %bitcast.68), calls=%async_computation.10 | async-start | bytes 8388608
  72.9 10.0 %slice-start.3 = ((s8[16777216]{0:T(1024)(128)(4,1)}), s8[4194304]{0:T(1024)(128)(4,1)S(1)}, s32[]{:S(2)}) async-start(s8[16777216]{0:T(1024)(128)(4,1)} %bitcast.68), calls=%async_computation.11 | async-start | bytes 8388608
  86.9 27.3 %all-to-all-start.1 = ((f32[8,8,4096]{2,1,0:T(8,128)}), f32[8,8,4096]{2,1,0:T(8,128)S(1)}, u32[]{:S(2)}, u32[]{:S(2)}) async-start(f32[8,8,4096]{2,1,0:T(8,128)} %fusion), calls=%async_computation.1 | async-start | bytes 2097152 | tf_op jit(solution)/shard_map/all_to_all | solution.py:105
  91.1 27.3 %copy-start.1 = (s32[28,2]{0,1:T(2,128)S(1)}, s32[28,2]{0,1:T(2,128)}, u32[]{:S(2)}) copy-start(s32[28,2]{0,1:T(2,128)} %param.9) | copy-start | bytes 676
  114.2 19.6 %all-to-all-start.3 = ((f32[8,8,4096]{2,1,0:T(8,128)}), f32[8,8,4096]{2,1,0:T(8,128)S(1)}, u32[]{:S(2)}, u32[]{:S(2)}) async-start(f32[8,8,4096]{2,1,0:T(8,128)} %fusion.15), calls=%async_computation.4 | async-start | bytes 2097152 | tf_op jit(solution)/shard_map/all_to_all | solution.py:112
  118.4 33.8 %reduce-scatter.3.cloned.1.call-start = ((), (), s32[]{:S(2)}) async-start(), calls=%async_computation.6 | async-start | bytes 327680 | tf_op jit(solution)/shard_map/reduce_scatter | solution.py:123
  120.1 15.1 %copy-start = (bf16[64,2048]{1,0:T(8,128)(2,1)S(1)}, bf16[64,2048]{1,0:T(8,128)(2,1)}, u32[]{:S(2)}) copy-start(bf16[64,2048]{1,0:T(8,128)(2,1)} %get-tuple-element.9) | copy-start | bytes 786436
  120.1 45.3 %reduce-scatter.5.cloned.1.call-start = ((), (), s32[]{:S(2)}) async-start(), calls=%async_computation.7 | async-start | bytes 327680 | tf_op jit(solution)/shard_map/reduce_scatter | solution.py:126
Sparse Core Ops, SparseCore 0:
  122.0 22.2 reduce-scatter.2
  147.1 18.1 reduce-scatter.4
where the time goes:
time: 173 us; the launch traced here: 172 us
  matrix products  88.6 us (51%)
  blocking collectives  31.7 us (18%)
  waiting for transfers between devices  17 us (10%)
  starting transfers between devices  16.4 us (9%)
  between operations  14.2 us (8%)
  local copies, waits for them, and re-layouts  3.7 us (2%)
    dot_general x3, matrix products, contract_cols(): lax.dot_general(left, right, (((1,), (1,)), ((), ())), preferred_element_...  34 us
    dot_general x5, matrix products, contract_rows(): lax.dot_general(left, right, (((0,), (0,)), ((), ())), preferred_element_...  29 us
    all_gather x1, blocking collectives, per_device(): lax.all_gather(scaled, 'tp', axis=1, tiled=True)  16.8 us
    all_gather x1, blocking collectives, per_device(): lax.all_gather(tokens, 'tp', axis=1, tiled=True)  14.9 us
    reduce_scatter x1, waiting for transfers between devices, per_device(): lax.psum_scatter(grad_tokens.astype(jnp.bfloat16), 'tp', scatter_dimensio...  13.1 us
    dot_general x1, matrix products, per_device(): jnp.dot(token_rows, gate_mat, preferred_element_type=jnp.float32)  9.95 us
    dot_general x1, matrix products, per_device(): hidden_up = jnp.dot(token_rows, up_mat, preferred_element_type=jnp.float32)  8.94 us
    all_to_all x1, starting transfers between devices, per_device(): lax.all_to_all(out_term.reshape(exp_devices, capacity, model_width), 'exp...  4.21 us
  transfers between devices with their start and end apart: 6, of which 2 were waited for; matrix products, arithmetic and copies ran while one was open for 38% of the time, Pallas kernels for 0%

commit v1 on v0

--- a/solution.py
+++ b/solution.py
@@ -5,6 +5,27 @@
 
 EXPERTS = 8
 CAP = 8
+
+
+def numbers_edit(piece_in, k_dim):
+    piece_in = jnp.moveaxis(piece_in, 0, k_dim)
+    g_now = piece_in.shape
+    return piece_in.reshape(*g_now[:k_dim], g_now[k_dim] * g_now[k_dim + 1], *g_now[k_dim + 2 :])
+
+
+def points_review(local_block, axis_key):
+    outer = lax.axis_size(axis_key)
+    known = lax.axis_index(axis_key)
+    tall, wide_out = (outer, known)
+    f_now, z_new = (local_block[None], 1)
+    while z_new < tall:
+        kept_arr = tuple(((j, j ^ z_new) for j in range(tall)))
+        t_next = lax.ppermute(f_now, axis_name=axis_key, perm=kept_arr)
+        carry_out = wide_out & z_new == 0
+        prior = jnp.where(carry_out, f_now, t_next)
+        f_now = jnp.concatenate([prior, jnp.where(carry_out, t_next, f_now)])
+        z_new *= 2
+    return f_now
 
 
 def contract_rows(left, right):
@@ -61,8 +82,11 @@
             preferred_element_type=jnp.float32,
         )
 
+    def report_trails_over_axis(chunk, on_dim, inner_x):
+        return numbers_edit(points_review(chunk, inner_x), on_dim)
+
     whole_tokens, whole_scaled = (
-        lax.all_gather(tokens, "tp", axis=1, tiled=True),
+        report_trails_over_axis(tokens, 1, "tp"),
         lax.all_gather(scaled, "tp", axis=1, tiled=True),
     )
     col_count = whole_tokens.shape[1]

time: 173 us -> 166 us (0.960)
  blocking collectives: 31.7 us -> 14.9 us
  waiting for transfers between devices: 17 us -> 22.8 us
  starting transfers between devices: 16.4 us -> 19.8 us
    all_gather x1 -> x0, blocking collectives: 14.9 us -> none  [per_device(): lax.all_gather(tokens, 'tp', axis=1, tiled=True)]
    all_to_all x1, waiting for transfers between devices: 0.01 us -> 5.82 us  [per_device(): lax.all_to_all(grad_send, 'exp', split_axis=0, concat_axis=0, tiled=True)]
    ppermute x0 -> x2, starting transfers between devices: none -> 3.9 us  [points_review(): t_next = lax.ppermute(f_now, axis_name=axis_key, perm=kept_arr)]
    all_gather x1, blocking collectives: 16.8 us -> 14.9 us  [per_device(): lax.all_gather(scaled, 'tp', axis=1, tiled=True)]
  transfers between devices with their start and end apart: 6 -> 8, of which waited for: 2 -> 4; matrix products, arithmetic and copies ran while one was open for 38% -> 42% of each run, Pallas kernels for 0% -> 0%
where the time goes in v1:
time: 166 us
  matrix products  88.6 us (53%)
  waiting for transfers between devices  22.8 us (14%)
  starting transfers between devices  19.8 us (12%)
  blocking collectives  14.9 us (9%)
  between operations  14.3 us (9%)
  local copies, waits for them, and re-layouts  4.06 us (2%)
    dot_general x3, matrix products, contract_cols(): lax.dot_general(left, right, (((1,), (1,)), ((), ())), preferred_element_...  34 us
    dot_general x5, matrix products, contract_rows(): lax.dot_general(left, right, (((0,), (0,)), ((), ())), preferred_element_...  29 us
    all_gather x1, blocking collectives, per_device(): lax.all_gather(scaled, 'tp', axis=1, tiled=True)  14.9 us
    reduce_scatter x1, waiting for transfers between devices, per_device(): lax.psum_scatter(grad_tokens.astype(jnp.bfloat16), 'tp', scatter_dimensio...  11.6 us
    dot_general x1, matrix products, per_device(): jnp.dot(token_rows, gate_mat, preferred_element_type=jnp.float32)  9.93 us
    dot_general x1, matrix products, per_device(): hidden_up = jnp.dot(token_rows, up_mat, preferred_element_type=jnp.float32)  8.94 us
    all_to_all x1, waiting for transfers between devices, per_device(): lax.all_to_all(grad_send, 'exp', split_axis=0, concat_axis=0, tiled=True)  5.82 us
    all_to_all x1, starting transfers between devices, per_device(): lax.all_to_all(back_term.reshape(exp_devices, capacity, model_width), 'ex...  4.2 us
  transfers between devices with their start and end apart: 8, of which 4 were waited for; matrix products, arithmetic and copies ran while one was open for 42% of the time, Pallas kernels for 0%

profile of v1, /device:TPU:0, one launch (start us, length us, event | category | flops | bytes accessed | tf_op | source)
XLA Modules:
  0.0 165.9 jit_solution(5571709557808271126)
XLA Ops:
  7.2 3.1 %collective-permute-start = (bf16[1,28,1024]{2,1,0:T(8,128)(2,1)}, bf16[1,28,1024]{2,1,0:T(8,128)(2,1)S(1)}, u32[]{:S(2)}, u32[]{:S(2)}) collective-permute-start(bf16[1,28,1024]{2,1,0:T(8,128)(2,1)} %bitcast.80), channel_id=1, source_target_pairs={{0,1},{1,0},{2,3},{3,2},{4,5},{5,4},{6,7},{7,6},{8,9},{9,8},{10,11... | collective-permute-start | bytes 172040 | tf_op jit(solution)/shard_map/ppermute | solution.py:23
  12.4 0.9 mul.79
  13.6 14.9 %all_gather.3 = bf16[56,4096]{1,0:T(8,128)(2,1)S(1)} all-gather(bf16[56,1024]{1,0:T(8,128)(2,1)S(1)} %multiply_convert_fusion.3), channel_id=1, replica_groups=mesh['exp'=8,'tp'=4] {'tp'}, dimensions={1}, use_global_device_ids=true | all-gather | bytes 573440 | tf_op jit(solution)/shard_map/all_gather | solution.py:90
  30.1 1.2 fusion.19
  31.3 3.7 %all-to-all-start.2 = ((bf16[8,8,4096]{2,1,0:T(8,128)(2,1)}), bf16[8,8,4096]{2,1,0:T(8,128)(2,1)S(1)}, u32[]{:S(2)}, u32[]{:S(2)}) async-start(bf16[8,8,4096]{2,1,0:T(8,128)(2,1)} %fusion.19), calls=%async_computation.3 | async-start | bytes 1048576 | tf_op jit(solution)/shard_map/all_to_all | solution.py:110
  35.2 1.5 collective-permute-done.1
  37.7 1.2 fusion.18
  38.9 5.8 %all-to-all-done.2 = bf16[8,8,4096]{2,1,0:T(8,128)(2,1)S(1)} async-done(((bf16[8,8,4096]{2,1,0:T(8,128)(2,1)}), bf16[8,8,4096]{2,1,0:T(8,128)(2,1)S(1)}, u32[]{:S(2)}, u32[]{:S(2)}) %all-to-all-start.2) | async-done | bytes 524320 | tf_op jit(solution)/shard_map/all_to_all | solution.py:110
  44.7 3.7 %all-to-all-start = ((bf16[8,8,4096]{2,1,0:T(8,128)(2,1)}), bf16[8,8,4096]{2,1,0:T(8,128)(2,1)S(1)}, u32[]{:S(2)}, u32[]{:S(2)}) async-start(bf16[8,8,4096]{2,1,0:T(8,128)(2,1)} %fusion.18), calls=%async_computation | async-start | bytes 1048576 | tf_op jit(solution)/shard_map/all_to_all | solution.py:109
  48.4 10.9 %fusion.2 = f32[64,2048]{1,0:T(8,128)S(1)} fusion(bf16[1,2048,4096]{2,1,0:T(8,128)(2,1)} %param.13, bf16[8,8,4096]{2,1,0:T(8,128)(2,1)S(1)} %all-to-all-done.2), kind=kOutput, calls=%fused_computation.2 | convolution fusion | flops 1073741824 | bytes 17825792 | tf_op jit(solution)/shard_map/dot_general | solution.py:38
  59.4 8.9 %fusion.6 = f32[64,2048]{1,0:T(8,128)S(1)} fusion(bf16[1,4096,2048]{2,1,0:T(8,128)(2,1)} %param.12, bf16[8,8,4096]{2,1,0:T(8,128)(2,1)S(1)} %all-to-all-done), kind=kOutput, calls=%fused_computation.6 | convolution fusion | flops 1073741824 | bytes 17825792 | tf_op jit(solution)/shard_map/dot_general | solution.py:115
  68.4 9.9 %multiply_convert_fusion.1 = (bf16[64,2048]{1,0:T(8,128)(2,1)}, bf16[64,2048]{1,0:T(8,128)(2,1)S(1)}, bf16[64,2048]{1,0:T(8,128)(2,1)}) fusion(f32[64,2048]{1,0:T(8,128)S(1)} %fusion.2, f32[64,2048]{1,0:T(8,128)S(1)} %fusion.6, bf16[1,4096,2048]{2,1,0:T(8,128)(2,1)} %param.11, bf16[8,8,4096]{2,1,0:T(8,128)(2,1)S(1)} %all-to-all-done), kind=kOutput, calls=%fused_computation.32 | convolution fusion | flops 1075838976 | bytes 19136512 | tf_op jit(solution)/shard_map/dot_general | solution.py:114
  78.3 4.0 %fusion = f32[8,8,4096]{2,1,0:T(8,128)} fusion(bf16[1,2048,4096]{2,1,0:T(8,128)(2,1)S(1)} %bitcast.77, bf16[64,2048]{1,0:T(8,128)(2,1)S(1)} %get-tuple-element.8), kind=kOutput, calls=%fused_computation | convolution fusion | flops 1073741824 | bytes 18087936 | tf_op jit(solution)/shard_map/dot_general | solution.py:119
  82.4 3.9 %all-to-all-start.1 = ((f32[8,8,4096]{2,1,0:T(8,128)}), f32[8,8,4096]{2,1,0:T(8,128)S(1)}, u32[]{:S(2)}, u32[]{:S(2)}) async-start(f32[8,8,4096]{2,1,0:T(8,128)} %fusion), calls=%async_computation.1 | async-start | bytes 2097152 | tf_op jit(solution)/shard_map/all_to_all | solution.py:129
  86.3 11.0 %fusion.4 = f32[64,4096]{1,0:T(8,128)S(1)} fusion(bf16[64,2048]{1,0:T(8,128)(2,1)} %get-tuple-element.9, bf16[1,4096,2048]{2,1,0:T(8,128)(2,1)} %param.12), kind=kOutput, calls=%fused_computation.4 | convolution fusion | flops 1073741824 | bytes 18087936 | tf_op jit(solution)/shard_map/dot_general | solution.py:38
  97.4 12.0 %fusion.15 = f32[8,8,4096]{2,1,0:T(8,128)} fusion(f32[64,4096]{1,0:T(8,128)S(1)} %fusion.4, bf16[64,2048]{1,0:T(8,128)(2,1)} %get-tuple-element.7, bf16[1,4096,2048]{2,1,0:T(8,128)(2,1)} %param.11), kind=kOutput, calls=%fused_computation.16 | convolution fusion | flops 1074003968 | bytes 19136512 | tf_op jit(solution)/shard_map/dot_general | solution.py:38
  109.4 4.2 %all-to-all-start.3 = ((f32[8,8,4096]{2,1,0:T(8,128)}), f32[8,8,4096]{2,1,0:T(8,128)S(1)}, u32[]{:S(2)}, u32[]{:S(2)}) async-start(f32[8,8,4096]{2,1,0:T(8,128)} %fusion.15), calls=%async_computation.4 | async-start | bytes 2097152 | tf_op jit(solution)/shard_map/all_to_all | solution.py:136
  113.9 1.3 convolution_convert_fusion.3
  115.6 9.5 %convert_bitcast_fusion.2 = bf16[1,4096,2048]{2,1,0:T(8,128)(2,1)} fusion(bf16[64,2048]{1,0:T(8,128)(2,1)} %get-tuple-element.7, bf16[8,8,4096]{2,1,0:T(8,128)(2,1)S(1)} %all-to-all-done), kind=kOutput, calls=%fused_computation.14 | convolution fusion | flops 1082130432 | bytes 17563648 | tf_op jit(solution)/shard_map/dot_general | solution.py:32
  125.1 3.9 %all-to-all-done.3 = f32[8,8,4096]{2,1,0:T(8,128)S(1)} async-done(((f32[8,8,4096]{2,1,0:T(8,128)}), f32[8,8,4096]{2,1,0:T(8,128)S(1)}, u32[]{:S(2)}, u32[]{:S(2)}) %all-to-all-start.3) | async-done | bytes 1048608 | tf_op jit(solution)/shard_map/all_to_all | solution.py:136
  129.0 1.3 convolution_convert_fusion.2
  130.3 8.5 %convert_bitcast_fusion.1 = bf16[1,4096,2048]{2,1,0:T(8,128)(2,1)} fusion(bf16[64,2048]{1,0:T(8,128)(2,1)S(1)} %copy-done, bf16[8,8,4096]{2,1,0:T(8,128)(2,1)S(1)} %all-to-all-done), kind=kOutput, calls=%fused_computation.13 | convolution fusion | flops 1082130432 | bytes 17563648 | tf_op jit(solution)/shard_map/dot_general | solution.py:32
  138.9 8.5 %convert_bitcast_fusion = bf16[1,2048,4096]{2,1,0:T(8,128)(2,1)} fusion(bf16[64,2048]{1,0:T(8,128)(2,1)S(1)} %get-tuple-element.8, bf16[8,8,4096]{2,1,0:T(8,128)(2,1)S(1)} %all-to-all-done.2), kind=kOutput, calls=%fused_computation.12 | convolution fusion | flops 1082130432 | bytes 17563648 | tf_op jit(solution)/shard_map/dot_general | solution.py:32
  147.4 11.6 %reduce-scatter.5.cloned.1.call-done = bf16[28,1024]{1,0:T(8,128)(2,1)} async-done(((bf16[28,4096]{1,0:T(8,128)(2,1)}), bf16[28,1024]{1,0:T(8,128)(2,1)}) %reduce-scatter.5.cloned.1.call-update) | async-done | bytes 57360 | tf_op jit(solution)/shard_map/reduce_scatter | solution.py:150
  (46 shorter events, 5.8 us)
Async XLA Ops:
  7.2 21.3 %collective-permute-start = (bf16[1,28,1024]{2,1,0:T(8,128)(2,1)}, bf16[1,28,1024]{2,1,0:T(8,128)(2,1)S(1)}, u32[]{:S(2)}, u32[]{:S(2)}) collective-permute-start(bf16[1,28,1024]{2,1,0:T(8,128)(2,1)} %bitcast.80), channel_id=1, source_target_pairs={{0,1},{1,0},{2,3},{3,2},{4,5},{5,4},{6,7},{7,6},{8,9},{9,8},{10,11... | collective-permute-start | bytes 172040 | tf_op jit(solution)/shard_map/ppermute | solution.py:23
  29.3 7.3 %collective-permute-start.1 = (bf16[2,28,1024]{2,1,0:T(8,128)(2,1)S(1)}, bf16[2,28,1024]{2,1,0:T(8,128)(2,1)S(1)}, u32[]{:S(2)}, u32[]{:S(2)}) collective-permute-start(bf16[2,28,1024]{2,1,0:T(8,128)(2,1)S(1)} %pad_maximum_fusion), channel_id=1, source_target_pairs={{0,2},{1,3},{2,0},{3,1},{4,6},{5,7},{6,4},{7,5},{8,10},{9,11},{10,... | collective-permute-start | bytes 344072 | tf_op jit(solution)/shard_map/ppermute | solution.py:23
  31.3 13.4 %all-to-all-start.2 = ((bf16[8,8,4096]{2,1,0:T(8,128)(2,1)}), bf16[8,8,4096]{2,1,0:T(8,128)(2,1)S(1)}, u32[]{:S(2)}, u32[]{:S(2)}) async-start(bf16[8,8,4096]{2,1,0:T(8,128)(2,1)} %fusion.19), calls=%async_computation.3 | async-start | bytes 1048576 | tf_op jit(solution)/shard_map/all_to_all | solution.py:110
  44.7 14.6 %all-to-all-start = ((bf16[8,8,4096]{2,1,0:T(8,128)(2,1)}), bf16[8,8,4096]{2,1,0:T(8,128)(2,1)S(1)}, u32[]{:S(2)}, u32[]{:S(2)}) async-start(bf16[8,8,4096]{2,1,0:T(8,128)(2,1)} %fusion.18), calls=%async_computation | async-start | bytes 1048576 | tf_op jit(solution)/shard_map/all_to_all | solution.py:109
  59.4 18.9 %slice-start = ((s8[16777216]{0:T(1024)(128)(4,1)}), s8[4194304]{0:T(1024)(128)(4,1)S(1)}, s32[]{:S(2)}) async-start(s8[16777216]{0:T(1024)(128)(4,1)} %bitcast.76), calls=%async_computation.8 | async-start | bytes 8388608
  59.4 18.9 %slice-start.1 = ((s8[16777216]{0:T(1024)(128)(4,1)}), s8[4194304]{0:T(1024)(128)(4,1)S(1)}, s32[]{:S(2)}) async-start(s8[16777216]{0:T(1024)(128)(4,1)} %bitcast.76), calls=%async_computation.9 | async-start | bytes 8388608
  68.3 10.0 %slice-start.2 = ((s8[16777216]{0:T(1024)(128)(4,1)}), s8[4194304]{0:T(1024)(128)(4,1)S(1)}, s32[]{:S(2)}) async-start(s8[16777216]{0:T(1024)(128)(4,1)} %bitcast.76), calls=%async_computation.10 | async-start | bytes 8388608
  68.4 10.0 %slice-start.3 = ((s8[16777216]{0:T(1024)(128)(4,1)}), s8[4194304]{0:T(1024)(128)(4,1)S(1)}, s32[]{:S(2)}) async-start(s8[16777216]{0:T(1024)(128)(4,1)} %bitcast.76), calls=%async_computation.11 | async-start | bytes 8388608
  82.4 27.0 %all-to-all-start.1 = ((f32[8,8,4096]{2,1,0:T(8,128)}), f32[8,8,4096]{2,1,0:T(8,128)S(1)}, u32[]{:S(2)}, u32[]{:S(2)}) async-start(f32[8,8,4096]{2,1,0:T(8,128)} %fusion), calls=%async_computation.1 | async-start | bytes 2097152 | tf_op jit(solution)/shard_map/all_to_all | solution.py:129
  86.3 27.3 %copy-start.1 = (s32[28,2]{0,1:T(2,128)S(1)}, s32[28,2]{0,1:T(2,128)}, u32[]{:S(2)}) copy-start(s32[28,2]{0,1:T(2,128)} %param.9) | copy-start | bytes 676
  109.4 19.6 %all-to-all-start.3 = ((f32[8,8,4096]{2,1,0:T(8,128)}), f32[8,8,4096]{2,1,0:T(8,128)S(1)}, u32[]{:S(2)}, u32[]{:S(2)}) async-start(f32[8,8,4096]{2,1,0:T(8,128)} %fusion.15), calls=%async_computation.4 | async-start | bytes 2097152 | tf_op jit(solution)/shard_map/all_to_all | solution.py:136
  113.6 33.8 %reduce-scatter.3.cloned.1.call-start = ((), (), s32[]{:S(2)}) async-start(), calls=%async_computation.6 | async-start | bytes 327680 | tf_op jit(solution)/shard_map/reduce_scatter | solution.py:147
  115.3 15.1 %copy-start = (bf16[64,2048]{1,0:T(8,128)(2,1)S(1)}, bf16[64,2048]{1,0:T(8,128)(2,1)}, u32[]{:S(2)}) copy-start(bf16[64,2048]{1,0:T(8,128)(2,1)} %get-tuple-element.9) | copy-start | bytes 786436
  115.3 43.7 %reduce-scatter.5.cloned.1.call-start = ((), (), s32[]{:S(2)}) async-start(), calls=%async_computation.7 | async-start | bytes 327680 | tf_op jit(solution)/shard_map/reduce_scatter | solution.py:150
Sparse Core Ops, SparseCore 0:
  117.2 20.6 reduce-scatter.2
  140.7 18.2 reduce-scatter.4
